TPU v7x, 256 devices: a whole 4x4x8 slice. The times are simulated.
256 devices in a mesh: dp: 32 (over x, z), tensor: 8 (over y, core).
Axes of the slice: x: 4, y: 4, z: 8, core: 2. Of those that a mesh axis runs over, the one named last changes fastest.
Arguments:
- vis_rows: bfloat16 [8, 256, 2, 3200], P(None, 'dp', None, 'tensor'), may hold values from -6 to 6
- ln_gain: float32 [2, 3200], replicated, may hold values from 0.25 to 1.75
- ln_bias: float32 [2, 3200], replicated, may hold values from -3 to 3
- proj_weight: bfloat16 [3200, 2, 8192], P('dp', None, 'tensor'), may hold values from -0.078125 to 0.078125
- text_rows: bfloat16 [32, 384, 8192], P('dp', None, 'tensor'), may hold values from -8 to 8
- attn_gain: float32 [8192], replicated, may hold values from 0.25 to 1.75
- w_query: bfloat16 [8192, 4096], P('dp', 'tensor'), may hold values from -0.088388348 to 0.088388348
- key_value_weight: bfloat16 [8192, 2, 1024], P('dp', None, 'tensor'), may hold values from -0.088388348 to 0.088388348
- tile_counts: int32 [32], replicated, may hold values from 1 to 16, 256 in all
- image_offsets: int32 [32], P('dp'), may hold values from 0 to 256
Outputs:
- attn_context: bfloat16 [32, 384, 4096], P('dp', None, 'tensor')
Inputs may be any that keep to these rules, and one draw needn't show every extreme that they name: tile_counts counts all 256 tiles, and its largest entry is exactly 16.
All inputs are finite; a program needn't handle non-finite values.
Results may differ from a plain program's by a relative error of at most 0.0074.
Values may be sent and summed in bfloat16 or wider, within the bound.
No kernel may reach another device: no remote copies, remote signals or barrier semaphores. Data moves between devices by JAX's collectives and lax.ppermute only.
A program may use at most 128 MiB of HBM per device.

v0:
```python
import jax
import jax.numpy as jnp
from jax import lax
from jax.sharding import PartitionSpec as P

QUERY_HEADS = 32
KEY_VALUE_HEADS = 8
HEAD_WIDTH = 128
vision_epsilon = 1e-06
decoder_epsilon = 1e-05
rope_base = 500000.0


def from_everyone(array, axis):
    count = lax.axis_size(axis)
    return lax.all_to_all(
        jnp.broadcast_to(array[None], (count, *array.shape)), axis, 0, 0, tiled=True
    )


def laid_out(tiles, dim):
    shape = list(tiles.shape[1:])
    shape[dim] *= tiles.shape[0]
    return jnp.moveaxis(tiles, 0, dim).reshape(shape)


def gather_directly(array, axis, dim):
    tiles = from_everyone(array, axis)
    return laid_out(tiles, dim)


def sent_together(arrays, axis, dim, along):
    columns = [a.reshape(*a.shape[:along], -1) for a in arrays]
    both = jnp.concatenate(columns, axis=along)
    filled, at, finished = (lax.all_gather(both, axis, axis=dim, tiled=True), 0, [])
    for a, column in zip(arrays, columns):
        piece = filled[..., at : at + column.shape[along]]
        finished.append(piece.reshape(*piece.shape[:along], *a.shape[along:]))
        at += column.shape[along]
    return tuple(finished)


def apply_rotary(value_rows, position_indices):
    half_width = value_rows.shape[-1] // 2
    exponents = jnp.arange(half_width, dtype=jnp.float32) * (2.0 / value_rows.shape[-1])
    frequency = rope_base ** (-exponents)
    angles = position_indices.astype(jnp.float32)[:, None] * frequency[None, :]
    cosine = jnp.cos(angles)[:, None, :]
    sine = jnp.sin(angles)[:, None, :]
    first_half = value_rows[..., :half_width]
    second_half = value_rows[..., half_width:]
    return jnp.concatenate(
        [first_half * cosine - second_half * sine, second_half * cosine + first_half * sine],
        axis=-1,
    )


def layer_norm(value_rows, gain, bias_values):
    average = jnp.mean(value_rows, axis=(-2, -1), keepdims=True)
    centered = value_rows - average
    variance = jnp.mean(centered * centered, axis=(-2, -1), keepdims=True)
    return centered * lax.rsqrt(variance + vision_epsilon) * gain + bias_values


def attend(query_full, key_value_complete):
    seq_len = query_full.shape[0]
    query_group_count = QUERY_HEADS // KEY_VALUE_HEADS
    local_kv = key_value_complete.shape[2] // HEAD_WIDTH
    local_query = query_full.shape[1] // HEAD_WIDTH
    position_indices = jnp.arange(seq_len, dtype=jnp.int32)
    query_rows = apply_rotary(
        query_full.reshape(seq_len, local_query, HEAD_WIDTH), position_indices
    ).astype(jnp.bfloat16)
    query_rows = query_rows.reshape(seq_len, local_kv, query_group_count, HEAD_WIDTH)
    key_rows = apply_rotary(
        key_value_complete[:, 0].reshape(seq_len, local_kv, HEAD_WIDTH), position_indices
    ).astype(jnp.bfloat16)
    value_rows = (
        key_value_complete[:, 1].reshape(seq_len, local_kv, HEAD_WIDTH).astype(jnp.bfloat16)
    )
    scores = jnp.einsum(
        "pgjd,kgd->gjpk", query_rows, key_rows, preferred_element_type=jnp.float32
    ) * HEAD_WIDTH ** (-0.5)
    causal = position_indices[:, None] >= position_indices[None, :]
    scores = jnp.where(causal[None, None], scores, -1e30)
    row_max = jnp.max(scores, axis=-1, keepdims=True)
    exponentials = jnp.exp(scores - row_max)
    weights = (exponentials / jnp.sum(exponentials, axis=-1, keepdims=True)).astype(jnp.bfloat16)
    context = jnp.einsum("gjpk,kgd->pgjd", weights, value_rows, preferred_element_type=jnp.float32)
    return context.astype(jnp.bfloat16).reshape(seq_len, local_query * HEAD_WIDTH)


def per_device(
    vis_rows,
    ln_gain,
    ln_bias,
    proj_weight,
    text_rows,
    attn_gain,
    w_query,
    key_value_weight,
    tile_counts,
    image_offsets,
):
    data_count = lax.axis_size("dp")
    data_index = lax.axis_index("dp")
    tile_rows, tile_tok, merge_count, part_width = vis_rows.shape
    vision_width = ln_gain.shape[1]
    part_model = proj_weight.shape[2]
    token_count = tile_rows * tile_tok
    max_tiles = 2 * tile_rows
    slot_count = (max_tiles + data_count - 1) // data_count
    tile_ends = jnp.cumsum(tile_counts)
    tile_firsts = tile_ends - tile_counts
    sample_ids = jnp.arange(data_count, dtype=jnp.int32)
    tiles_here = jnp.arange(tile_rows, dtype=jnp.int32) * data_count + data_index
    owners = jnp.sum((tile_ends[None, :] <= tiles_here[:, None]).astype(jnp.int32), axis=1)
    owner_first = jnp.sum(
        jnp.where(sample_ids[None, :] == owners[:, None], tile_firsts[None, :], 0), axis=1
    )
    slots = (tiles_here - owner_first) // data_count
    is_mine = sample_ids == data_index
    my_first = jnp.sum(jnp.where(is_mine, tile_firsts, 0))
    my_count = jnp.sum(jnp.where(is_mine, tile_counts, 0))
    tile_order = jnp.arange(max_tiles, dtype=jnp.int32)
    sources = (my_first + tile_order) % data_count
    slot_index = tile_order // data_count
    image_span = max_tiles * tile_tok
    whole = gather_directly(vis_rows, "tensor", 3)
    merged = whole.reshape(token_count, merge_count, vision_width).astype(jnp.float32)
    normed_vis = layer_norm(merged, ln_gain, ln_bias).astype(jnp.bfloat16)
    columns = normed_vis
    image_cols = (
        jnp.einsum(
            "rmf,fmo->ro",
            columns,
            lax.all_gather(proj_weight, "dp", axis=0, tiled=True),
            preferred_element_type=jnp.float32,
        )
        .astype(jnp.bfloat16)
        .reshape(tile_rows, tile_tok, part_model)
    )
    empty_slots = jnp.zeros((data_count, slot_count) + image_cols.shape[1:], jnp.bfloat16)
    received = lax.all_to_all(
        empty_slots.at[owners, slots].set(image_cols), "dp", split_axis=0, concat_axis=0, tiled=True
    )
    arrived = received[sources, slot_index]
    arrived = arrived.reshape(image_span, part_model)
    start_row = image_offsets[0]
    sequence = text_rows[0]
    current = lax.dynamic_slice_in_dim(sequence, start_row, image_span, 0)
    is_image = jnp.repeat(tile_order < my_count, tile_tok)[:, None]
    combined = jnp.where(is_image, arrived, current)
    sequence = lax.dynamic_update_slice_in_dim(sequence, combined, start_row, 0)
    gathered = gather_directly(sequence, "tensor", 1)
    seq_float = gathered.astype(jnp.float32)
    mean_square = jnp.mean(seq_float * seq_float, axis=-1, keepdims=True)
    normalized_sequence = (seq_float * lax.rsqrt(mean_square + decoder_epsilon) * attn_gain).astype(
        jnp.bfloat16
    )
    seq_len = normalized_sequence.shape[0]
    weight_rows = sent_together((w_query, key_value_weight), "dp", 0, 1)
    columns = normalized_sequence
    query_part = jnp.dot(columns, weight_rows[0], preferred_element_type=jnp.float32)
    keyval_part = jnp.einsum(
        "sd,dck->sck", columns, weight_rows[1], preferred_element_type=jnp.float32
    )
    context = attend(query_part, keyval_part)
    return context.reshape(1, seq_len, context.shape[1])


def solution(mesh):
    in_specs = (
        P(None, "dp", None, "tensor"),
        P(),
        P(),
        P("dp", None, "tensor"),
        P("dp", None, "tensor"),
        P(),
        P("dp", "tensor"),
        P("dp", None, "tensor"),
        P(),
        P("dp"),
    )
    out_specs = P("dp", None, "tensor")
    return jax.shard_map(
        per_device, mesh=mesh, in_specs=in_specs, out_specs=out_specs, check_vma=False
    )
```

profile of v0, /device:TPU:1, one launch (start us, length us, event | category | flops | bytes accessed | tf_op | source)
XLA Modules:
  0.0 314.7 jit_solution(18428205670531530554)
XLA Ops:
  6.5 1.2 copy.86
  7.8 0.9 copy.81
  9.6 1.1 broadcast_in_dim.55
  10.7 6.7 %all-to-all-start = ((bf16[8,8,8,2,400]{4,2,1,3,0:T(8,128)(2,1)}), bf16[8,8,8,2,400]{4,2,1,3,0:T(8,128)(2,1)S(1)}, u32[]{:S(2)}, u32[]{:S(2)}) async-start(bf16[8,8,8,2,400]{4,2,1,3,0:T(8,128)(2,1)} %broadcast_in_dim.55), calls=%async_computation | async-start | bytes 2097152 | tf_op jit(solution)/shard_map/all_to_all | solution.py:16
  18.7 13.6 %all-to-all-done = bf16[8,8,8,2,400]{4,2,1,3,0:T(8,128)(2,1)S(1)} async-done(((bf16[8,8,8,2,400]{4,2,1,3,0:T(8,128)(2,1)}), bf16[8,8,8,2,400]{4,2,1,3,0:T(8,128)(2,1)S(1)}, u32[]{:S(2)}, u32[]{:S(2)}) %all-to-all-start) | async-done | bytes 819232 | tf_op jit(solution)/shard_map/all_to_all | solution.py:16
  33.6 1.6 copy.53
  35.2 2.3 reshape.465
  37.5 97.1 %all-gather.3.cloned.1.call-done = bf16[3200,2,1024]{2,1,0:T(2,128)(2,1)} async-done(((bf16[100,2,1024]{2,1,0:T(2,128)(2,1)}), bf16[3200,2,1024]{2,1,0:T(2,128)(2,1)}) %all-gather.3.cloned.1.call-update) | async-done | bytes 13107216 | tf_op jit(solution)/shard_map/all_gather | solution.py:137
  134.6 9.4 %fusion.16 = bf16[8,8,1024]{2,1,0:T(8,128)(2,1)S(1)} fusion(bf16[3200,2,1024]{2,1,0:T(2,128)(2,1)} %all-gather.3.cloned.1.call-done, f32[64,2,3200]{2,0,1:T(8,128)} %reshape.465, f32[2,3200]{1,0:T(2,128)S(1)} %copy-done.5, f32[2,3200]{1,0:T(2,128)S(1)} %copy-done.6, f32[64]{0:T(128)S(1)} %rsqrt.20, f32[64]{0:T(128)S(1)} %div.47), kind=kOutput, calls=%fused_computation.24 | convolution fusion | flops 840974336 | bytes 14928384 | tf_op jit(solution)/shard_map/rmf,fmo->ro/dot_general | solution.py:134
  144.9 2.1 scatter_fusion
  147.0 5.3 %all-to-all-start.1 = ((bf16[32,1,8,1024]{3,2,1,0:T(8,128)(2,1)}), bf16[32,1,8,1024]{3,2,1,0:T(8,128)(2,1)S(1)}, u32[]{:S(2)}, u32[]{:S(2)}) async-start(bf16[32,1,8,1024]{3,2,1,0:T(8,128)(2,1)} %bitcast.8), calls=%async_computation.1 | async-start | bytes 1048576 | tf_op jit(solution)/shard_map/all_to_all | solution.py:144
  154.5 17.5 %all-to-all-done.1 = bf16[32,1,8,1024]{3,2,1,0:T(8,128)(2,1)S(1)} async-done(((bf16[32,1,8,1024]{3,2,1,0:T(8,128)(2,1)}), bf16[32,1,8,1024]{3,2,1,0:T(8,128)(2,1)S(1)}, u32[]{:S(2)}, u32[]{:S(2)}) %all-to-all-start.1) | async-done | bytes 524320 | tf_op jit(solution)/shard_map/all_to_all | solution.py:144
  172.7 1.8 dynamic_update_slice.5
  174.5 3.4 %broadcast_in_dim.61 = bf16[8,384,1024]{2,1,0:T(8,128)(2,1)} broadcast(bf16[384,1024]{1,0:T(8,128)(2,1)S(1)} %dynamic_update_slice.5), dimensions={1,2} | broadcast | bytes 7077888 | tf_op jit(solution)/shard_map/broadcast_in_dim | solution.py:17
  177.9 8.6 %all-to-all-start.2 = ((bf16[8,384,1024]{2,1,0:T(8,128)(2,1)}), bf16[8,384,1024]{2,1,0:T(8,128)(2,1)}, u32[]{:S(2)}, u32[]{:S(2)}) async-start(bf16[8,384,1024]{2,1,0:T(8,128)(2,1)} %broadcast_in_dim.61), calls=%async_computation.2 | async-start | bytes 12582912 | tf_op jit(solution)/shard_map/all_to_all | solution.py:16
  187.0 74.0 %all-gather.5.cloned.1.call-done = bf16[8192,768]{1,0:T(8,128)(2,1)} async-done(((bf16[256,768]{1,0:T(8,128)(2,1)}), bf16[8192,768]{1,0:T(8,128)(2,1)}) %all-gather.5.cloned.1.call-update) | async-done | bytes 12582928 | tf_op jit(solution)/shard_map/all_gather | solution.py:35
  261.0 7.1 %slice_bitcast_fusion = bf16[512,8192]{0,1:T(8,128)(2,1)} fusion(bf16[8192,768]{1,0:T(8,128)(2,1)} %all-gather.5.cloned.1.call-done), kind=kLoop, calls=%fused_computation.9 | loop fusion | bytes 16777216 | tf_op jit(solution)/shard_map/dot_general | solution.py:164
  268.1 11.9 %copy.58 = bf16[512,8192]{1,0:T(8,128)(2,1)} copy(bf16[512,8192]{0,1:T(8,128)(2,1)} %slice_bitcast_fusion) | data formatting | bytes 16777216 | tf_op jit(solution)/shard_map/dot_general | solution.py:164
  280.0 8.7 %copy.55 = bf16[8,384,1024]{1,2,0:T(8,128)(2,1)} copy(bf16[8,384,1024]{2,1,0:T(8,128)(2,1)} %all-to-all-done.2) | data formatting | bytes 12582912 | tf_op jit(solution)/shard_map/all_to_all | solution.py:16
  288.7 4.3 %fusion.2 = f32[384]{0:T(512)S(1)} fusion(bf16[8,384,1024]{1,2,0:T(8,128)(2,1)} %copy.55), kind=kLoop, calls=%fused_computation.6 | loop fusion | flops 9436800 | bytes 6292992 | tf_op jit(solution)/shard_map/reduce_sum | solution.py:157
  293.3 1.7 fusion.4
  295.0 4.8 %fusion.5 = f32[384,256]{0,1:S(1)} fusion(bf16[384,8192]{0,1:T(8,128)(2,1)S(1)} %bitcast.102, bf16[8192,768]{1,0:T(8,128)(2,1)} %all-gather.5.cloned.1.call-done), kind=kOutput, calls=%fused_computation.10 | convolution fusion | flops 1610612736 | bytes 10878976
  300.3 4.5 %fusion.56 = f32[384,4,128]{0,2,1:T(8,128)S(1)} fusion(bf16[384,8192,1]{0,1,2:T(8,128)(2,1)S(1)} %bitcast.103, bf16[4,128,8192]{2,1,0:T(8,128)(2,1)S(1)} %bitcast.101), kind=kOutput, calls=%fused_computation.102 | convolution fusion | flops 3221225472 | bytes 15466496 | tf_op jit(solution)/shard_map/dot_general | solution.py:164
  306.9 0.9 copy.63
  (59 shorter events, 9.8 us)
Async XLA Ops:
  6.5 3.0 copy-start.2
  6.5 2.2 copy-start.1
  6.5 128.0 %all-gather.3.cloned.1.call-start = ((), (), s32[]{:S(2)}) async-start(), calls=%async_computation.3 | async-start | bytes 13516800 | tf_op jit(solution)/shard_map/all_gather | solution.py:137
  7.8 253.2 %all-gather.5.cloned.1.call-start = ((), (), s32[]{:S(2)}) async-start(), calls=%async_computation.4 | async-start | bytes 12976128 | tf_op jit(solution)/shard_map/all_gather | solution.py:35
  8.7 8.6 %copy-start.4 = (s32[32]{0:T(128)S(1)}, s32[32]{0:T(128)}, u32[]{:S(2)}) copy-start(s32[32]{0:T(128)} %param.18) | copy-start | bytes 388
  10.7 21.7 %all-to-all-start = ((bf16[8,8,8,2,400]{4,2,1,3,0:T(8,128)(2,1)}), bf16[8,8,8,2,400]{4,2,1,3,0:T(8,128)(2,1)S(1)}, u32[]{:S(2)}, u32[]{:S(2)}) async-start(bf16[8,8,8,2,400]{4,2,1,3,0:T(8,128)(2,1)} %broadcast_in_dim.55), calls=%async_computation | async-start | bytes 2097152 | tf_op jit(solution)/shard_map/all_to_all | solution.py:16
  35.2 99.4 %copy-start.5 = (f32[2,3200]{1,0:T(2,128)S(1)}, f32[2,3200]{1,0:T(2,128)}, u32[]{:S(2)}) copy-start(f32[2,3200]{1,0:T(2,128)} %param.12) | copy-start | bytes 76804
  35.2 99.4 %copy-start.6 = (f32[2,3200]{1,0:T(2,128)S(1)}, f32[2,3200]{1,0:T(2,128)}, u32[]{:S(2)}) copy-start(f32[2,3200]{1,0:T(2,128)} %param.11) | copy-start | bytes 76804
  147.0 25.0 %all-to-all-start.1 = ((bf16[32,1,8,1024]{3,2,1,0:T(8,128)(2,1)}), bf16[32,1,8,1024]{3,2,1,0:T(8,128)(2,1)S(1)}, u32[]{:S(2)}, u32[]{:S(2)}) async-start(bf16[32,1,8,1024]{3,2,1,0:T(8,128)(2,1)} %bitcast.8), calls=%async_computation.1 | async-start | bytes 1048576 | tf_op jit(solution)/shard_map/all_to_all | solution.py:144
  177.9 8.6 %copy-start.3 = (f32[8192]{0:T(1024)S(1)}, f32[8192]{0:T(1024)}, u32[]{:S(2)}) copy-start(f32[8192]{0:T(1024)} %param.15) | copy-start | bytes 98308
  177.9 102.1 %all-to-all-start.2 = ((bf16[8,384,1024]{2,1,0:T(8,128)(2,1)}), bf16[8,384,1024]{2,1,0:T(8,128)(2,1)}, u32[]{:S(2)}, u32[]{:S(2)}) async-start(bf16[8,384,1024]{2,1,0:T(8,128)(2,1)} %broadcast_in_dim.61), calls=%async_computation.2 | async-start | bytes 12582912 | tf_op jit(solution)/shard_map/all_to_all | solution.py:16
  288.7 4.6 %copy-start = (bf16[8,384,1024]{1,2,0:T(8,128)(2,1)S(1)}, bf16[8,384,1024]{1,2,0:T(8,128)(2,1)}, u32[]{:S(2)}) copy-start(bf16[8,384,1024]{1,2,0:T(8,128)(2,1)} %copy.55) | copy-start | bytes 18874372
  293.3 7.0 %slice-start = ((s8[8388608]{0:T(1024)(128)(4,1)}), s8[4194304]{0:T(1024)(128)(4,1)S(1)}, s32[]{:S(2)}) async-start(s8[8388608]{0:T(1024)(128)(4,1)} %bitcast.99), calls=%async_computation.5 | async-start | bytes 8388608
  295.0 5.2 %slice-start.1 = ((s8[8388608]{0:T(1024)(128)(4,1)}), s8[4194304]{0:T(1024)(128)(4,1)S(1)}, s32[]{:S(2)}) async-start(s8[8388608]{0:T(1024)(128)(4,1)} %bitcast.99), calls=%async_computation.6 | async-start | bytes 8388608
Sparse Core Ops, SparseCore 0:
  9.9 124.6 all-gather.2
  137.2 123.7 all-gather.4
where the time goes:
time: 316 us; the launch traced here: 315 us
  waiting for transfers between devices  202 us (64%)
  local copies, waits for them, and re-layouts  45.2 us (14%)
  starting transfers between devices  20.6 us (7%)
  matrix products  20.2 us (6%)
  between operations  14.3 us (5%)
  other arithmetic  12.2 us (4%)
    all_gather x1, waiting for transfers between devices, per_device(): lax.all_gather(proj_weight, 'dp', axis=0, tiled=True)  97.1 us
    all_gather x1, waiting for transfers between devices, sent_together(): lax.all_gather(both, axis, axis=dim, tiled=True)  74 us
    dot_general x2, local copies, waits for them, and re-layouts, per_device(): jnp.dot(columns, weight_rows[0], preferred_element_type=jnp.float32)  19 us
    all_to_all x1, waiting for transfers between devices, per_device(): lax.all_to_all(empty_slots.at[owners, slots].set(image_cols), 'dp', split...  17.5 us
    all_to_all x2, starting transfers between devices, from_everyone(): lax.all_to_all(jnp.broadcast_to(array[None], (count, *array.shape)), axis...  15.2 us
    all_to_all x2, waiting for transfers between devices, from_everyone(): lax.all_to_all(jnp.broadcast_to(array[None], (count, *array.shape)), axis...  13.6 us
    dot_general x1, matrix products, per_device(): jnp.einsum('rmf,fmo->ro', columns, lax.all_gather(proj_weight, 'dp', axis...  9.42 us
    all_to_all x1, local copies, waits for them, and re-layouts, from_everyone(): lax.all_to_all(jnp.broadcast_to(array[None], (count, *array.shape)), axis...  8.65 us
  transfers between devices with their start and end apart: 5, of which 4 were waited for; matrix products, arithmetic and copies ran while one was open for 15% of the time, Pallas kernels for 0%

commit v1 on v0

--- a/solution.py
+++ b/solution.py
@@ -9,6 +9,14 @@
 vision_epsilon = 1e-06
 decoder_epsilon = 1e-05
 rope_base = 500000.0
+
+
+def gather_from_all(array, axis, dim):
+    size = lax.axis_size(axis)
+    repeats = [size if d == dim else 1 for d in range(array.ndim)]
+    return lax.all_to_all(
+        jnp.tile(array, repeats), axis, split_axis=dim, concat_axis=dim, tiled=True
+    )
 
 
 def from_everyone(array, axis):
@@ -134,7 +142,7 @@
         jnp.einsum(
             "rmf,fmo->ro",
             columns,
-            lax.all_gather(proj_weight, "dp", axis=0, tiled=True),
+            gather_from_all(proj_weight, "dp", 0),
             preferred_element_type=jnp.float32,
         )
         .astype(jnp.bfloat16)

time: 316 us -> 576 us (1.82)
  waiting for transfers between devices: 202 us -> 420 us
  blocking collectives: 0 us -> 20.7 us
  local copies, waits for them, and re-layouts: 45.2 us -> 57.1 us
  starting transfers between devices: 20.6 us -> 30 us
    all_to_all x0 -> x1, waiting for transfers between devices: none -> 358 us  [gather_from_all(): lax.all_to_all(jnp.tile(array, repeats), axis, split_axis=dim, concat_axi...]
    all_gather x1 -> x0, waiting for transfers between devices: 97.1 us -> none  [per_device(): lax.all_gather(proj_weight, 'dp', axis=0, tiled=True)]
    all_gather x1, waiting for transfers between devices: 74 us -> 0.02 us  [sent_together(): lax.all_gather(both, axis, axis=dim, tiled=True)]
    all_to_all x2 -> x1, waiting for transfers between devices: 13.6 us -> 51.7 us  [from_everyone(): lax.all_to_all(jnp.broadcast_to(array[None], (count, *array.shape)), axis...]
    all_to_all x0 -> x1, blocking collectives: none -> 20.7 us  [from_everyone(): lax.all_to_all(jnp.broadcast_to(array[None], (count, *array.shape)), axis...]
    another operation x1 -> x2, local copies, waits for them, and re-layouts: 0.09 us -> 13 us  [the longest x1 12.9 us: gather_from_all(): jnp.tile(array, repeats)]
    all_to_all x0 -> x1, starting transfers between devices: none -> 11.3 us  [gather_from_all(): lax.all_to_all(jnp.tile(array, repeats), axis, split_axis=dim, concat_axi...]
    all_to_all x1, waiting for transfers between devices: 17.5 us -> 10.9 us  [per_device(): lax.all_to_all(empty_slots.at[owners, slots].set(image_cols), 'dp', split...]
  transfers between devices with their start and end apart: 5 -> 4, of which waited for: 4 -> 3; matrix products, arithmetic and copies ran while one was open for 15% -> 8% of each run, Pallas kernels for 0% -> 0%
where the time goes in v1:
time: 576 us; the launch traced here: 575 us
  waiting for transfers between devices  420 us (73%)
  local copies, waits for them, and re-layouts  57.1 us (10%)
  starting transfers between devices  30 us (5%)
  blocking collectives  20.7 us (4%)
  matrix products  20.2 us (4%)
  between operations  14.3 us (2%)
  other arithmetic  12.2 us (2%)
    all_to_all x1, waiting for transfers between devices, gather_from_all(): lax.all_to_all(jnp.tile(array, repeats), axis, split_axis=dim, concat_axi...  358 us
    all_to_all x1, waiting for transfers between devices, from_everyone(): lax.all_to_all(jnp.broadcast_to(array[None], (count, *array.shape)), axis...  51.7 us
    all_to_all x1, blocking collectives, from_everyone(): lax.all_to_all(jnp.broadcast_to(array[None], (count, *array.shape)), axis...  20.7 us
    dot_general x2, local copies, waits for them, and re-layouts, per_device(): jnp.dot(columns, weight_rows[0], preferred_element_type=jnp.float32)  19 us
    another operation x1, local copies, waits for them, and re-layouts, gather_from_all(): jnp.tile(array, repeats)  12.9 us
  transfers between devices with their start and end apart: 4, of which 3 were waited for; matrix products, arithmetic and copies ran while one was open for 8% of the time, Pallas kernels for 0%

profile of v1, /device:TPU:1, one launch (start us, length us, event | category | flops | bytes accessed | tf_op | source)
XLA Modules:
  0.0 574.8 jit_solution(11031413764469781988)
XLA Ops:
  6.5 1.2 copy.94
  7.7 0.9 copy.56
  8.7 20.7 %all_to_all.20 = bf16[8,8,8,2,400]{4,2,1,3,0:T(8,128)(2,1)S(1)} all-to-all(bf16[8,8,8,2,400]{4,2,1,3,0:T(8,128)(2,1)S(1)} %broadcast_in_dim.55), channel_id=1, replica_groups=mesh['dp'=32,'tensor'=8] {'tensor'}, dimensions={0} | all-to-all | bytes 1638400 | tf_op jit(solution)/shard_map/all_to_all | solution.py:24
  29.4 12.9 %tile.4.clone = bf16[32,100,2,1024]{3,2,1,0:T(2,128)(2,1)} broadcast(bf16[100,2,1024]{2,1,0:T(2,128)(2,1)S(1)} %copy-done.1), dimensions={1,2,3} | broadcast | bytes 13516800 | tf_op jit(solution)/shard_map/tile | solution.py:18
  42.4 11.3 %all-to-all-start.1 = ((bf16[3200,2,1024]{2,1,0:T(2,128)(2,1)}), bf16[3200,2,1024]{2,1,0:T(2,128)(2,1)}, u32[]{:S(2)}, u32[]{:S(2)}) async-start(bf16[3200,2,1024]{2,1,0:T(2,128)(2,1)} %bitcast.99), calls=%async_computation.1 | async-start | bytes 26214400 | tf_op jit(solution)/shard_map/all_to_all | solution.py:17
  57.1 1.6 copy.57
  58.8 2.2 reshape.469
  61.0 357.8 %all-to-all-done.1 = bf16[3200,2,1024]{2,1,0:T(2,128)(2,1)} async-done(((bf16[3200,2,1024]{2,1,0:T(2,128)(2,1)}), bf16[3200,2,1024]{2,1,0:T(2,128)(2,1)}, u32[]{:S(2)}, u32[]{:S(2)}) %all-to-all-start.1) | async-done | bytes 13107232 | tf_op jit(solution)/shard_map/all_to_all | solution.py:17
  418.9 9.4 %fusion.16 = bf16[8,8,1024]{2,1,0:T(8,128)(2,1)S(1)} fusion(bf16[3200,2,1024]{2,1,0:T(2,128)(2,1)} %all-to-all-done.1, f32[64,2,3200]{2,0,1:T(8,128)} %reshape.469, f32[2,3200]{1,0:T(2,128)S(1)} %copy-done.6, f32[2,3200]{1,0:T(2,128)S(1)} %copy-done.7, f32[64]{0:T(128)S(1)} %rsqrt.20, f32[64]{0:T(128)S(1)} %div.47), kind=kOutput, calls=%fused_computation.24 | convolution fusion | flops 840974336 | bytes 14928384 | tf_op jit(solution)/shard_map/rmf,fmo->ro/dot_general | solution.py:142
  429.2 2.1 scatter_fusion
  431.3 8.8 %all-to-all-start.2 = ((bf16[32,1,8,1024]{3,2,1,0:T(8,128)(2,1)}), bf16[32,1,8,1024]{3,2,1,0:T(8,128)(2,1)S(1)}, u32[]{:S(2)}, u32[]{:S(2)}) async-start(bf16[32,1,8,1024]{3,2,1,0:T(8,128)(2,1)} %bitcast.9), calls=%async_computation.2 | async-start | bytes 1048576 | tf_op jit(solution)/shard_map/all_to_all | solution.py:152
  442.2 10.9 %all-to-all-done.2 = bf16[32,1,8,1024]{3,2,1,0:T(8,128)(2,1)S(1)} async-done(((bf16[32,1,8,1024]{3,2,1,0:T(8,128)(2,1)}), bf16[32,1,8,1024]{3,2,1,0:T(8,128)(2,1)S(1)}, u32[]{:S(2)}, u32[]{:S(2)}) %all-to-all-start.2) | async-done | bytes 524320 | tf_op jit(solution)/shard_map/all_to_all | solution.py:152
  453.8 1.8 dynamic_update_slice.5
  455.5 3.4 broadcast_in_dim.61
  458.9 9.9 %all-to-all-start.3 = ((bf16[8,384,1024]{2,1,0:T(8,128)(2,1)}), bf16[8,384,1024]{2,1,0:T(8,128)(2,1)}, u32[]{:S(2)}, u32[]{:S(2)}) async-start(bf16[8,384,1024]{2,1,0:T(8,128)(2,1)} %broadcast_in_dim.61), calls=%async_computation.3 | async-start | bytes 12582912 | tf_op jit(solution)/shard_map/all_to_all | solution.py:24
  469.4 7.1 %slice_bitcast_fusion = bf16[512,8192]{0,1:T(8,128)(2,1)} fusion(bf16[8192,768]{1,0:T(8,128)(2,1)} %all-gather.2.cloned.1.call-done), kind=kLoop, calls=%fused_computation.9 | loop fusion | bytes 16777216 | tf_op jit(solution)/shard_map/dot_general | solution.py:172
  476.5 11.9 %copy.64 = bf16[512,8192]{1,0:T(8,128)(2,1)} copy(bf16[512,8192]{0,1:T(8,128)(2,1)} %slice_bitcast_fusion) | data formatting | bytes 16777216 | tf_op jit(solution)/shard_map/dot_general | solution.py:172
  488.4 51.7 %all-to-all-done.3 = bf16[8,384,1024]{2,1,0:T(8,128)(2,1)} async-done(((bf16[8,384,1024]{2,1,0:T(8,128)(2,1)}), bf16[8,384,1024]{2,1,0:T(8,128)(2,1)}, u32[]{:S(2)}, u32[]{:S(2)}) %all-to-all-start.3) | async-done | bytes 6291488 | tf_op jit(solution)/shard_map/all_to_all | solution.py:24
  540.1 8.7 %copy.61 = bf16[8,384,1024]{1,2,0:T(8,128)(2,1)} copy(bf16[8,384,1024]{2,1,0:T(8,128)(2,1)} %all-to-all-done.3) | data formatting | bytes 12582912 | tf_op jit(solution)/shard_map/all_to_all | solution.py:24
  548.7 4.3 fusion.2
  553.3 1.7 fusion.4
  555.1 4.8 fusion.5
  560.4 4.5 fusion.56
  567.0 0.9 copy.69
  (60 shorter events, 9.9 us)
Async XLA Ops:
  6.5 22.9 %copy-start.1 = (bf16[100,2,1024]{2,1,0:T(2,128)(2,1)S(1)}, bf16[100,2,1024]{2,1,0:T(2,128)(2,1)}, u32[]{:S(2)}) copy-start(bf16[100,2,1024]{2,1,0:T(2,128)(2,1)} %param.13) | copy-start | bytes 1228804
  42.4 11.4 %copy-start.3 = (bf16[256,2,128]{2,1,0:T(2,128)(2,1)S(1)}, bf16[256,2,128]{2,1,0:T(2,128)(2,1)}, u32[]{:S(2)}) copy-start(bf16[256,2,128]{2,1,0:T(2,128)(2,1)} %param.17) | copy-start | bytes 393220
  42.4 11.4 %copy-start.2 = (bf16[256,512]{1,0:T(8,128)(2,1)S(1)}, bf16[256,512]{1,0:T(8,128)(2,1)}, u32[]{:S(2)}) copy-start(bf16[256,512]{1,0:T(8,128)(2,1)} %param.16) | copy-start | bytes 786436
  42.4 12.2 %copy-start.5 = (s32[32]{0:T(128)S(1)}, s32[32]{0:T(128)}, u32[]{:S(2)}) copy-start(s32[32]{0:T(128)} %param.18) | copy-start | bytes 388
  42.4 376.5 %all-to-all-start.1 = ((bf16[3200,2,1024]{2,1,0:T(2,128)(2,1)}), bf16[3200,2,1024]{2,1,0:T(2,128)(2,1)}, u32[]{:S(2)}, u32[]{:S(2)}) async-start(bf16[3200,2,1024]{2,1,0:T(2,128)(2,1)} %bitcast.99), calls=%async_computation.1 | async-start | bytes 26214400 | tf_op jit(solution)/shard_map/all_to_all | solution.py:17
  53.7 415.7 %all-gather.2.cloned.1.call-start = ((), (), s32[]{:S(2)}) async-start(), calls=%async_computation.4 | async-start | bytes 12976128 | tf_op jit(solution)/shard_map/all_gather | solution.py:43
  58.8 360.1 %copy-start.6 = (f32[2,3200]{1,0:T(2,128)S(1)}, f32[2,3200]{1,0:T(2,128)}, u32[]{:S(2)}) copy-start(f32[2,3200]{1,0:T(2,128)} %param.12) | copy-start | bytes 76804
  58.8 360.0 %copy-start.7 = (f32[2,3200]{1,0:T(2,128)S(1)}, f32[2,3200]{1,0:T(2,128)}, u32[]{:S(2)}) copy-start(f32[2,3200]{1,0:T(2,128)} %param.11) | copy-start | bytes 76804
  431.3 21.8 %all-to-all-start.2 = ((bf16[32,1,8,1024]{3,2,1,0:T(8,128)(2,1)}), bf16[32,1,8,1024]{3,2,1,0:T(8,128)(2,1)S(1)}, u32[]{:S(2)}, u32[]{:S(2)}) async-start(bf16[32,1,8,1024]{3,2,1,0:T(8,128)(2,1)} %bitcast.9), calls=%async_computation.2 | async-start | bytes 1048576 | tf_op jit(solution)/shard_map/all_to_all | solution.py:152
  458.9 9.9 %copy-start.4 = (f32[8192]{0:T(1024)S(1)}, f32[8192]{0:T(1024)}, u32[]{:S(2)}) copy-start(f32[8192]{0:T(1024)} %param.15) | copy-start | bytes 98308
  458.9 81.2 %all-to-all-start.3 = ((bf16[8,384,1024]{2,1,0:T(8,128)(2,1)}), bf16[8,384,1024]{2,1,0:T(8,128)(2,1)}, u32[]{:S(2)}, u32[]{:S(2)}) async-start(bf16[8,384,1024]{2,1,0:T(8,128)(2,1)} %broadcast_in_dim.61), calls=%async_computation.3 | async-start | bytes 12582912 | tf_op jit(solution)/shard_map/all_to_all | solution.py:24
  548.7 4.6 copy-start
  553.3 7.0 %slice-start = ((s8[8388608]{0:T(1024)(128)(4,1)}), s8[4194304]{0:T(1024)(128)(4,1)S(1)}, s32[]{:S(2)}) async-start(s8[8388608]{0:T(1024)(128)(4,1)} %bitcast.100), calls=%async_computation.5 | async-start | bytes 8388608
  555.1 5.2 slice-start.1
Sparse Core Ops, SparseCore 0:
  57.1 300.5 all-gather.1
